TPU v7x, 32 devices: a whole 2x2x4 slice. The times are simulated.
32 devices in a mesh: ep: 4 (over y, x), fsdp: 8 (over z, core).
Axes of the slice: x: 2, y: 2, z: 4, core: 2. Of those that a mesh axis runs over, the one named last changes fastest.
Arguments:
- train_gate: float32 [64, 2048, 1408], P('ep', 'fsdp'), may hold values from -0.1875 to 0.1875
- other_gate: bfloat16 [64, 2048, 1408], P('ep', 'fsdp'), may hold values from -0.0625 to 0.0625
- train_up: float32 [64, 2048, 1408], P('ep', 'fsdp'), may hold values from -0.1875 to 0.1875
- other_up: bfloat16 [64, 2048, 1408], P('ep', 'fsdp'), may hold values from -0.0625 to 0.0625
- router_weight: float32 [2048, 64], P('fsdp', 'ep'), may hold values from -0.125 to 0.125
- router_gain: float32 [2048], P('fsdp'), may hold values from 0.25 to 1.75
Outputs:
- ready_gate: bfloat16 [64, 2048, 1408], P('ep', None, 'fsdp')
- ready_up: bfloat16 [64, 2048, 1408], P('ep', None, 'fsdp')
- scale_gate: float32 [64, 1408], P('ep', 'fsdp')
- scale_up: float32 [64, 1408], P('ep', 'fsdp')
- serve_router: bfloat16 [2048, 64], replicated
All inputs are finite; a program needn't handle non-finite values. Where the computation divides by a largest or mean magnitude, that divisor is 1e-20 or more.
Results may differ from a plain program's by a relative error of at most 0.001.
Values may be sent and summed in bfloat16 or wider, within the bound.
No kernel may reach another device: no remote copies, remote signals or barrier semaphores. Data moves between devices by JAX's collectives and lax.ppermute only.
A program may use at most 192 MiB of HBM per device.

v0:
```python
import jax
import jax.numpy as jnp
from jax import lax
from jax.sharding import PartitionSpec as P


def per_device(train_gate, other_gate, train_up, other_up, router_weight, router_gain):
    latest_gate = train_gate + other_gate.astype(jnp.float32)
    latest_up = train_up + other_up.astype(jnp.float32)
    scale_gate, scale_up = lax.pmax(
        (jnp.max(jnp.abs(latest_gate), axis=1), jnp.max(jnp.abs(latest_up), axis=1)), "fsdp"
    )
    narrow_gate, narrow_up = (
        (latest_gate / jnp.expand_dims(scale_gate, 1)).astype(jnp.bfloat16),
        (latest_up / jnp.expand_dims(scale_up, 1)).astype(jnp.bfloat16),
    )
    ready_gate, ready_up = (
        lax.all_to_all(narrow_gate, "fsdp", split_axis=2, concat_axis=1, tiled=True),
        lax.all_to_all(narrow_up, "fsdp", split_axis=2, concat_axis=1, tiled=True),
    )
    scale_gate = lax.dynamic_slice_in_dim(
        scale_gate, lax.axis_index("fsdp") * ready_gate.shape[2], ready_gate.shape[2], axis=1
    )
    scale_up = lax.dynamic_slice_in_dim(
        scale_up, lax.axis_index("fsdp") * ready_up.shape[2], ready_up.shape[2], axis=1
    )
    part_router = (router_weight * router_gain[:, None]).astype(jnp.bfloat16)
    row_router = lax.all_gather(part_router, "fsdp", axis=0, tiled=True)
    serve_router = lax.all_gather(row_router, "ep", axis=1, tiled=True)
    return (ready_gate, ready_up, scale_gate, scale_up, serve_router)


def solution(mesh):
    in_specs = (
        P("ep", "fsdp", None),
        P("ep", "fsdp", None),
        P("ep", "fsdp", None),
        P("ep", "fsdp", None),
        P("fsdp", "ep"),
        P("fsdp"),
    )
    out_specs = (
        P("ep", None, "fsdp"),
        P("ep", None, "fsdp"),
        P("ep", "fsdp"),
        P("ep", "fsdp"),
        P(),
    )
    return jax.shard_map(
        per_device, mesh=mesh, in_specs=in_specs, out_specs=out_specs, check_vma=False
    )
```

profile of v0, /device:TPU:0, one launch (start us, length us, event | category | flops | bytes accessed | tf_op | source)
XLA Modules:
  0.0 809.5 jit_solution(1631548331659294860)
XLA Ops:
  7.2 0.0 all-reduce.3.cloned.1.call-start
  7.2 23.7 %copy.38 = f32[16,256,1408]{1,0,2:T(8,128)} copy(f32[16,256,1408]{2,1,0:T(8,128)} %param.8) | data formatting | bytes 46137344 | tf_op args[2]
  30.9 16.4 %copy.37 = bf16[16,256,1408]{1,0,2:T(8,128)(2,1)} copy(bf16[16,256,1408]{2,1,0:T(8,128)(2,1)} %param.9) | data formatting | bytes 23068672 | tf_op args[3]
  47.2 23.7 %copy.34 = f32[16,256,1408]{1,0,2:T(8,128)} copy(f32[16,256,1408]{2,1,0:T(8,128)} %param.6) | data formatting | bytes 46137344 | tf_op args[0]
  70.9 16.4 %copy.33 = bf16[16,256,1408]{1,0,2:T(8,128)(2,1)} copy(bf16[16,256,1408]{2,1,0:T(8,128)(2,1)} %param.7) | data formatting | bytes 23068672 | tf_op args[1]
  87.3 0.0 copy-start
  87.3 0.0 copy-start.1
  87.3 20.8 %abs_reduce_fusion = f32[16,1408]{0,1:T(8,128)} fusion(f32[16,256,1408]{1,0,2:T(8,128)} %copy.38, bf16[16,256,1408]{1,0,2:T(8,128)(2,1)} %copy.37), kind=kLoop, calls=%fused_computation.1 | loop fusion | flops 23046144 | bytes 34693120 | tf_op jit(solution)/shard_map/reduce_max | solution.py:11
  108.1 0.0 copy-done
  108.1 0.0 copy-done.1
  108.1 14.9 %abs_reduce_fusion.1 = f32[16,1408]{0,1:T(8,128)} fusion(f32[16,256,1408]{1,0,2:T(8,128)S(1)} %copy-done, bf16[16,256,1408]{1,0,2:T(8,128)(2,1)S(1)} %copy-done.1), kind=kLoop, calls=%fused_computation.4 | loop fusion | flops 23046144 | bytes 34693120 | tf_op jit(solution)/shard_map/reduce_max | solution.py:11
  123.0 0.0 all-reduce.3.cloned.1.call-update
  123.0 64.1 %all-reduce.3.cloned.1.call-done = (f32[16,1408]{0,1:T(8,128)}, f32[16,1408]{0,1:T(8,128)}) async-done(((f32[16,1408]{0,1:T(8,128)}, f32[16,1408]{0,1:T(8,128)}), (f32[16,1408]{0,1:T(8,128)}, f32[16,1408]{0,1:T(8,128)})) %all-reduce.3.cloned.1.call-update) | async-done | bytes 180240 | tf_op jit(solution)/shard_map/pmax | solution.py:10
  187.2 27.3 %divide_convert_fusion = (bf16[16,256,1408]{1,0,2:T(8,128)(2,1)}, bf16[16,256,1408]{1,0,2:T(8,128)(2,1)S(1)}) fusion(f32[16,256,1408]{1,0,2:T(8,128)} %copy.38, bf16[16,256,1408]{1,0,2:T(8,128)(2,1)} %copy.37, f32[16,1408]{0,1:T(8,128)} %get-tuple-element.11, f32[16,1408]{0,1:T(8,128)} %get-tuple-element.10, f32[16,256,1408]{1,0,2:T(8,128)} %copy.34, ...), kind=kLoop, calls=%fused_computation | loop fusion | flops 46137344 | bytes 92454912 | tf_op jit(solution)/shard_map/convert_element_type | solution.py:15
  214.5 0.0 copy-start.2
  214.5 0.0 copy-start.3
  214.5 255.0 %all_to_all.36 = bf16[16,256,1408]{1,0,2:T(8,128)(2,1)} all-to-all(bf16[16,256,1408]{1,0,2:T(8,128)(2,1)S(1)} %get-tuple-element.13), channel_id=1, replica_groups=mesh['ep'=4,'fsdp'=8] {'fsdp'}, dimensions={2} | all-to-all | bytes 23068672 | tf_op jit(solution)/shard_map/all_to_all | solution.py:18
  469.5 5.3 all-to-all-start.1
  474.8 0.0 copy-done.2
  474.8 0.0 copy-done.3
  474.8 257.3 %all_gather.6 = bf16[2048,16]{0,1:T(8,128)(2,1)S(1)} all-gather(bf16[256,16]{0,1:T(8,128)(2,1)S(1)} %multiply_convert_fusion), channel_id=1, replica_groups=mesh['ep'=4,'fsdp'=8] {'fsdp'}, dimensions={0}, use_global_device_ids=true | all-gather | bytes 73728 | tf_op jit(solution)/shard_map/all_gather | solution.py:28
  732.1 8.9 %all_gather.7 = bf16[2048,64]{0,1:T(8,128)(2,1)S(1)} all-gather(bf16[2048,16]{0,1:T(8,128)(2,1)S(1)} %all_gather.6), channel_id=1, replica_groups=mesh['ep'=4,'fsdp'=8] {'ep'}, dimensions={1}, use_global_device_ids=true | all-gather | bytes 327680 | tf_op jit(solution)/shard_map/all_gather | solution.py:29
  741.0 0.9 constant_dynamic-slice_fusion
  742.0 0.7 copy.41
  742.6 0.7 copy.42
  743.3 11.3 %copy.36 = bf16[16,8,256,176]{2,1,3,0:T(8,128)(2,1)} copy(bf16[16,8,256,176]{2,0,3,1:T(8,128)(2,1)} %bitcast.14) | data formatting | bytes 23068672 | tf_op jit(solution)/shard_map/all_to_all | solution.py:18
  754.7 18.0 %all_to_all.29 = bf16[16,2048,176]{1,2,0:T(8,128)(2,1)} reshape(bf16[16,8,256,176]{2,1,3,0:T(8,128)(2,1)} %copy.36) | data formatting | bytes 23068672 | tf_op jit(solution)/shard_map/all_to_all | solution.py:18
  772.6 0.0 all-to-all-done.1
  772.6 11.4 %copy.40 = bf16[16,8,256,176]{2,1,3,0:T(8,128)(2,1)} copy(bf16[16,8,256,176]{2,0,3,1:T(8,128)(2,1)} %bitcast.5) | data formatting | bytes 23068672 | tf_op jit(solution)/shard_map/all_to_all | solution.py:19
  784.0 18.0 %all_to_all.33 = bf16[16,2048,176]{1,2,0:T(8,128)(2,1)} reshape(bf16[16,8,256,176]{2,1,3,0:T(8,128)(2,1)} %copy.40) | data formatting | bytes 23068672 | tf_op jit(solution)/shard_map/all_to_all | solution.py:19
  802.0 0.7 copy.48
  (1 shorter events, 0.0 us)
Async XLA Ops:
  7.2 180.0 %all-reduce.3.cloned.1.call-start = ((), (), s32[]{:S(2)}) async-start(), calls=%async_computation.2 | async-start | bytes 2883584 | tf_op jit(solution)/shard_map/pmax | solution.py:10
  87.3 20.8 %copy-start = (f32[16,256,1408]{1,0,2:T(8,128)S(1)}, f32[16,256,1408]{1,0,2:T(8,128)}, u32[]{:S(2)}) copy-start(f32[16,256,1408]{1,0,2:T(8,128)} %copy.34) | copy-start | bytes 69206016
  87.3 20.9 %copy-start.1 = (bf16[16,256,1408]{1,0,2:T(8,128)(2,1)S(1)}, bf16[16,256,1408]{1,0,2:T(8,128)(2,1)}, u32[]{:S(2)}) copy-start(bf16[16,256,1408]{1,0,2:T(8,128)(2,1)} %copy.33) | copy-start | bytes 34603012
  214.5 260.3 %copy-start.2 = (f32[256,16]{0,1:T(8,128)S(1)}, f32[256,16]{0,1:T(8,128)}, u32[]{:S(2)}) copy-start(f32[256,16]{0,1:T(8,128)} %param.10) | copy-start | bytes 49156
  214.5 260.3 %copy-start.3 = (f32[256]{0:T(256)S(1)}, f32[256]{0:T(256)}, u32[]{:S(2)}) copy-start(f32[256]{0:T(256)} %param.11) | copy-start | bytes 3076
  469.5 303.1 %all-to-all-start.1 = ((bf16[16,256,1408]{1,0,2:T(8,128)(2,1)}), bf16[16,256,1408]{1,0,2:T(8,128)(2,1)}, u32[]{:S(2)}, u32[]{:S(2)}) async-start(bf16[16,256,1408]{1,0,2:T(8,128)(2,1)} %get-tuple-element.12), calls=%async_computation.1 | async-start | bytes 23068672 | tf_op jit(solution)/shard_map/all_to_all | solution.py:19
Sparse Core Ops, SparseCore 0:
  123.2 63.9 all-reduce.2
where the time goes:
time: 812 us; the launch traced here: 810 us
  blocking collectives  521 us (64%)
  local copies, waits for them, and re-layouts  142 us (17%)
  waiting for transfers between devices  64.2 us (8%)
  other arithmetic  63 us (8%)
  between operations  14.1 us (2%)
    all_gather x1, blocking collectives, per_device(): row_router = lax.all_gather(part_router, 'fsdp', axis=0, tiled=True)  257 us
    all_to_all x1, blocking collectives, per_device(): lax.all_to_all(narrow_gate, 'fsdp', split_axis=2, concat_axis=1, tiled=True)  255 us
    unnamed x15, local copies, waits for them, and re-layouts  82.2 us
    pmax x1, waiting for transfers between devices, per_device(): lax.pmax((jnp.max(jnp.abs(latest_gate), axis=1), jnp.max(jnp.abs(latest_u...  64.1 us
    all_to_all x2, local copies, waits for them, and re-layouts, per_device(): lax.all_to_all(narrow_up, 'fsdp', split_axis=2, concat_axis=1, tiled=True)  29.3 us
    all_to_all x2, local copies, waits for them, and re-layouts, per_device(): lax.all_to_all(narrow_gate, 'fsdp', split_axis=2, concat_axis=1, tiled=True)  29.3 us
    convert_element_type x1, other arithmetic, per_device(): (latest_up / jnp.expand_dims(scale_up, 1)).astype(jnp.bfloat16)  27.3 us
    reduce_max x1, other arithmetic, per_device(): jnp.max(jnp.abs(latest_up), axis=1)  20.8 us
  transfers between devices with their start and end apart: 2, of which 1 were waited for; matrix products, arithmetic and copies ran while one was open for 2% of the time, Pallas kernels for 0%

commit v1 on v0

v1 whole, which is shorter than its diff:
```python
import jax
import jax.numpy as jnp
from jax import lax
from jax.experimental import pallas as pl
from jax.experimental.pallas import tpu as pltpu
from jax.sharding import PartitionSpec as P


HEAD = (1, 1)
BODY = (2, 4, 4, 3, 1)

ANY = pl.BlockSpec(memory_space=pl.ANY)
HBM = pl.BlockSpec(memory_space=pltpu.HBM)


def cost(flops, nbytes):
    return pl.CostEstimate(flops=flops, bytes_accessed=nbytes, transcendentals=0)


def latest(t, o):
    return t[0] + o[0].astype(jnp.float32)


def make(mesh):
    parts = mesh.shape["fsdp"]
    order = far_first(parts)

    def swap(x, k):
        return lax.ppermute(x, "fsdp", [(i, i ^ k) for i in range(parts)])

    def per_device(tg, og, tu, ou, router_weight, router_gain):
        experts, rows, cols = tg.shape
        width = cols // parts
        arrays = (tg, og, tu, ou)
        me = lax.axis_index("fsdp").astype(jnp.int32).reshape(1)
        smem = pl.BlockSpec(memory_space=pltpu.SMEM)

        def weights(e0):
            return [pl.BlockSpec((1, rows, cols), lambda e: (e0 + e, 0, 0))] * 4

        def peaks(e0, n, after, copies=1):
            def body(tg, og, tu, ou, *rest):
                out = rest[-1]
                e = pl.program_id(0)
                for m, (t, o) in enumerate(((tg, og), (tu, ou))):
                    top = jnp.max(jnp.abs(latest(t, o)), axis=0, keepdims=True)
                    for c in range(copies):
                        out[c, m, pl.ds(e, 1), :] = top

            return pl.pallas_call(
                body,
                grid=(n,),
                in_specs=weights(e0) + [ANY] * len(after),
                out_specs=pl.BlockSpec((copies, 2, n, cols), lambda e: (0, 0, 0, 0)),
                out_shape=jax.ShapeDtypeStruct((copies, 2, n, cols), jnp.float32),
                cost_estimate=cost(n * 3000000, n * rows * cols * 12),
                name="peaks",
            )(*arrays, *after)

        def pair_top(x, y):
            def body(me, x, y, out):
                c = me[0] & 1
                out[...] = jnp.maximum(x[c], y[c])

            return pl.pallas_call(
                body,
                in_specs=[smem] + [pl.BlockSpec(memory_space=pltpu.VMEM)] * 2,
                out_shape=jax.ShapeDtypeStruct(x.shape[1:], jnp.float32),
                name="pair_top",
            )(me, x, y)

        def all_top(xs, after):
            def body(*refs):
                top = refs[0][...]
                for r in refs[1 : len(xs)]:
                    top = jnp.maximum(top, r[...])
                refs[-1][...] = top

            return pl.pallas_call(
                body,
                in_specs=[pl.BlockSpec(memory_space=pltpu.VMEM)] * len(xs)
                + [ANY] * len(after),
                out_shape=jax.ShapeDtypeStruct(xs[0].shape, jnp.float32),
                name="all_top",
            )(*xs, *after)

        def exchange_start(peak):
            half = pair_top(peak, swap(peak, 1))
            far = [swap(half, k) for k in range(parts - 2, 0, -2)]
            return half, far

        def exchange_end(half, far, after):
            top = all_top([half] + far, after)
            return top, swap(top, 1)

        def ready(e0, n, row0, tops, after, whole=False):
            count = 1 if whole else parts
            paired = tops[0].ndim == 2

            def body(me, tg, og, tu, ou, *rest):
                outs, scale, turned = rest[-count - 2 : -2], rest[-2], rest[-1]
                e = pl.program_id(0)
                who = me[0]
                if paired:
                    even = (who & 1) == 0
                    a, b = (r[pl.ds(row0 + e, 1), :] for r in rest[:2])
                    top = (jnp.where(even, a, b), jnp.where(even, b, a))
                else:
                    top = []
                    for m in range(2):
                        t = rest[0][0, m, pl.ds(row0 + e, 1), :]
                        for d in range(1, parts):
                            t = jnp.maximum(t, rest[0][d, m, pl.ds(row0 + e, 1), :])
                        top.append(t)
                for m, (t, o) in enumerate(((tg, og), (tu, ou))):
                    scale[m, pl.ds(e, 1), :] = top[m]
                    value = (latest(t, o) / top[m]).astype(jnp.bfloat16).T
                    for d in range(parts):
                        block = value[d * width : (d + 1) * width]
                        if whole:
                            outs[0][d, m, 0] = block
                        else:
                            turned[d] = block
                    if not whole:
                        for k in range(parts):
                            outs[k][m, 0] = turned[who ^ k]

            block, shape = blocks_of(n, whole)
            small = [pl.BlockSpec(t.shape, lambda e, r=t.ndim: (0,) * r) for t in tops]
            res = pl.pallas_call(
                body,
                grid=(n,),
                in_specs=[smem] + weights(e0) + small + [ANY] * len(after),
                out_specs=[block] * count
                + [pl.BlockSpec((2, n, cols), lambda e: (0, 0, 0))],
                out_shape=[shape] * count
                + [jax.ShapeDtypeStruct((2, n, cols), jnp.float32)],
                scratch_shapes=[pltpu.VMEM((parts, width, rows), jnp.bfloat16)],
                cost_estimate=cost(n * 6000000, n * rows * cols * 16),
                name="ready",
            )(me, *arrays, *tops, *after)
            return res[:count], res[count]

        def blocks_of(n, whole):
            shape, at = (2, n, width, rows), (lambda e: (0, e, 0, 0))
            if whole:
                shape, at = (parts,) + shape, (lambda e: (0, 0, e, 0, 0))
            block = shape[:-3] + (1,) + shape[-2:]
            return pl.BlockSpec(block, at), jax.ShapeDtypeStruct(shape, jnp.bfloat16)

        def send(blocks):
            got = [blocks[0]] + [None] * (parts - 1)
            for k in order:
                got[k] = swap(blocks[k], k)
            return got

        def place(e0, n, got, full, after):
            whole = pl.BlockSpec((1, width, parts * rows), lambda e: (e0 + e, 0, 0))
            block = blocks_of(n, len(got) == 1)[0]
            shape = jax.ShapeDtypeStruct((experts, width, parts * rows), jnp.bfloat16)

            def body(me, *refs):
                ins, (gate, up) = refs[: len(got)], refs[-2:]
                for d in range(parts if len(got) == 1 else 0):
                    gate[0, :, d * rows : (d + 1) * rows] = ins[0][d, 0, 0]
                    up[0, :, d * rows : (d + 1) * rows] = ins[0][d, 1, 0]
                for k in range(parts if len(got) > 1 else 0):
                    at = pl.ds(pl.multiple_of((me[0] ^ k) * rows, rows), rows)
                    gate[0, :, at] = ins[k][0, 0]
                    up[0, :, at] = ins[k][1, 0]

            return pl.pallas_call(
                body,
                grid=(n,),
                in_specs=[smem] + [block] * len(got) + [ANY] * (len(full) + len(after)),
                out_specs=[whole, whole],
                out_shape=[shape, shape],
                input_output_aliases={1 + len(got) + i: i for i in range(len(full))},
                cost_estimate=cost(n * 3000000, n * rows * cols * 8),
                name="place",
            )(me, *got, *full, *after)

        def join(parts_of, after):
            def body(me, *refs):
                for k in range(parts):
                    at = pl.ds(pl.multiple_of((me[0] ^ k) * rows, rows), rows)
                    refs[-1][:, at] = refs[k][...]

            return pl.pallas_call(
                body,
                in_specs=[smem] + [pl.BlockSpec(memory_space=pltpu.VMEM)] * parts
                + [ANY] * len(after),
                out_shape=jax.ShapeDtypeStruct((parts_of[0].shape[0], parts * rows), jnp.bfloat16),
                name="join",
            )(me, *parts_of, *after)

        head, tail = groups(experts)
        h = sum(head)
        scales, flights = [], []

        def fly(i, e0, n, row0, tops, after):
            whole = i == 0
            blocks, scale = ready(e0, n, row0, tops, after, whole)
            scales.append(scale)
            got = [regroup(blocks[0])] if whole else send(blocks)
            flights.append((e0, n, got))
            return scale

        def regroup(x):
            return lax.all_to_all(x, "fsdp", split_axis=0, concat_axis=0, tiled=True)

        tops = (regroup(peaks(0, h, (), parts)),)
        at = fly(0, 0, head[0], 0, tops, ())
        rest = peaks(h, experts - h, (at,))
        rest = exchange_start(rest[0])
        e0 = head[0]
        for i, n in enumerate(head[1:], 1):
            at = fly(i, e0, n, e0, tops, (rest[0], at))
            e0 += n

        part_router = (router_weight * router_gain[:, None]).astype(jnp.bfloat16).T
        routers = [part_router] + [swap(part_router, k) for k in range(1, parts)]

        tops = exchange_end(*rest, (at,))
        for i, n in enumerate(tail, len(head)):
            at = fly(i, e0, n, e0 - h, tops, (at,))
            e0 += n

        scale = jnp.concatenate(scales, axis=1)
        scale = lax.dynamic_slice_in_dim(scale, lax.axis_index("fsdp") * width, width, axis=2)

        def keep(x):
            def body(x, out):
                out[...] = x[...]

            return pl.pallas_call(body, out_shape=jax.ShapeDtypeStruct(x.shape, x.dtype), name="keep")(x)

        full = ()
        for i, (e0, n, got) in enumerate(flights):
            after = ()
            if i == 2:
                serve_router = lax.all_gather(join(routers, full[:1]), "ep", axis=0, tiled=True)
                serve_router = keep(serve_router)
                after = (serve_router, scale)
            full = place(e0, n, got, full, after)
        gate, up = full
        return (
            jnp.swapaxes(gate, 1, 2),
            jnp.swapaxes(up, 1, 2),
            scale[0],
            scale[1],
            serve_router.T,
        )

    return per_device


def groups(experts):
    if sum(HEAD) + sum(BODY) == experts:
        return HEAD, BODY
    return (1, 1), (1,) * (experts - 2)


def far_first(parts):
    return [k + i for k in range(parts - 2, 0, -2) for i in (0, 1)] + [1]


def solution(mesh):
    in_specs = (P("ep", "fsdp", None),) * 4 + (P("fsdp", "ep"), P("fsdp"))
    out_specs = (P("ep", None, "fsdp"),) * 2 + (P("ep", "fsdp"),) * 2 + (P(),)
    body = make(mesh)

    def run(*args):
        mapped = jax.shard_map(
            body, mesh=mesh, in_specs=in_specs, out_specs=out_specs, check_vma=False
        )
        return mapped(*args)

    return run
```

time: 812 us -> 640 us (0.79)
  the two profiles are of different devices: /device:TPU:0 before, /device:TPU:8 now
where the time goes in v1:
time: 640 us; the launch traced here: 639 us
  waiting for transfers between devices  435 us (68%)
  Pallas kernels  103 us (16%)
  starting transfers between devices  72.8 us (11%)
  local copies, waits for them, and re-layouts  16.9 us (3%)
  blocking collectives  10.6 us (2%)
    ppermute x54, waiting for transfers between devices, swap(): return lax.ppermute(x, 'fsdp', [(i, i ^ k) for i in range(parts)])  429 us
    ppermute x54, starting transfers between devices, swap(): return lax.ppermute(x, 'fsdp', [(i, i ^ k) for i in range(parts)])  60.2 us
    pallas_call x7, Pallas kernels, ready(): pl.pallas_call(body, grid=(n,), in_specs=[smem] + weights(e0) + small + [...  43.3 us
    pallas_call x7, Pallas kernels, place(): pl.pallas_call(body, grid=(n,), in_specs=[smem] + [block] * len(got) + [A...  28.2 us
    pallas_call x2, Pallas kernels, peaks(): pl.pallas_call(body, grid=(n,), in_specs=weights(e0) + [ANY] * len(after)...  24.9 us
  transfers between devices with their start and end apart: 56, of which 26 were waited for; matrix products, arithmetic and copies ran while one was open for 1% of the time, Pallas kernels for 11%

profile of v1, /device:TPU:8, one launch (start us, length us, event | category | flops | bytes accessed | tf_op | source)
XLA Modules:
  0.0 639.1 jit_solution(9692568313680461235)
XLA Ops:
  0.6 4.4 peaks.2
  5.0 5.3 all-to-all-start
  10.4 6.4 %all-to-all-done.rest_0_ = f32[8,2,2,1408]{3,2,1,0:T(2,128)S(1)} async-done(((f32[8,2,2,1408]{3,2,1,0:T(2,128)}), f32[8,2,2,1408]{3,2,1,0:T(2,128)S(1)}, u32[]{:S(2)}, u32[]{:S(2)}) %all-to-all-start) | async-done | bytes 180256 | tf_op jit(solution)/shard_map/all_to_all | solution.py:210
  21.3 20.5 %peaks.3 = f32[1,2,14,1408]{3,2,1,0:T(8,128)} custom-call(f32[16,256,1408]{2,1,0:T(8,128)} %tg.17, bf16[16,256,1408]{2,1,0:T(8,128)(2,1)} %og.17, f32[16,256,1408]{2,1,0:T(8,128)} %tu.17, bf16[16,256,1408]{2,1,0:T(8,128)(2,1)} %ou.17, f32[2,1,1408]{2,1,0:T(1,128)} %get-tuple-element.75.rest_0_.rest_2_), custom_call_target="tpu_custom_call" | custom-call | flops 42000000 | bytes 60555264 | tf_op jit(solution)/shard_map/peaks/pallas_call | solution.py:50
  79.2 5.3 ready.9
  90.0 7.4 %collective-permute-done.44.refs_5_ = bf16[2,1,176,256]{3,2,1,0:T(8,128)(2,1)S(1)} collective-permute-done((bf16[2,1,176,256]{3,2,1,0:T(8,128)(2,1)}, bf16[2,1,176,256]{3,2,1,0:T(8,128)(2,1)S(1)}, u32[]{:S(2)}, u32[]{:S(2)}) %collective-permute-start.44) | collective-permute-done | bytes 180256 | tf_op jit(solution)/shard_map/ppermute | solution.py:29
  100.6 9.2 %ready.10 = (bf16[2,4,176,256]{3,2,1,0:T(8,128)(2,1)}, bf16[2,4,176,256]{3,2,1,0:T(8,128)(2,1)}, bf16[2,4,176,256]{3,2,1,0:T(8,128)(2,1)}, bf16[2,4,176,256]{3,2...) custom-call(s32[1]{0:T(128)} %bitcast.me, ...), custom_call_target="tpu_custom_call" | custom-call | flops 24000000 | bytes 23068672 | tf_op jit(solution)/shard_map/ready/pallas_call | solution.py:130
  109.8 9.3 %ready.11 = (bf16[2,4,176,256]{3,2,1,0:T(8,128)(2,1)}, bf16[2,4,176,256]{3,2,1,0:T(8,128)(2,1)}, bf16[2,4,176,256]{3,2,1,0:T(8,128)(2,1)}, bf16[2,4,176,256]{3,2...) custom-call(s32[1]{0:T(128)} %bitcast.me, ...), custom_call_target="tpu_custom_call" | custom-call | flops 24000000 | bytes 23068672 | tf_op jit(solution)/shard_map/ready/pallas_call | solution.py:130
  119.1 8.1 %ready.12 = (bf16[2,3,176,256]{3,2,1,0:T(8,128)(2,1)}, bf16[2,3,176,256]{3,2,1,0:T(8,128)(2,1)}, bf16[2,3,176,256]{3,2,1,0:T(8,128)(2,1)}, bf16[2,3,176,256]{3,2...) custom-call(s32[1]{0:T(128)} %bitcast.me, ...), custom_call_target="tpu_custom_call" | custom-call | flops 18000000 | bytes 17301504 | tf_op jit(solution)/shard_map/ready/pallas_call | solution.py:130
  133.8 5.8 collective-permute-done.6.refs_2_
  144.8 35.7 %collective-permute-done.36.refs_4_ = bf16[2,2,176,256]{3,2,1,0:T(8,128)(2,1)S(1)} collective-permute-done((bf16[2,2,176,256]{3,2,1,0:T(8,128)(2,1)S(1)}, bf16[2,2,176,256]{3,2,1,0:T(8,128)(2,1)S(1)}, u32[]{:S(2)}, u32[]{:S(2)}) %collective-permute-start.36) | collective-permute-done | bytes 360480 | tf_op jit(solution)/shard_map/ppermute | solution.py:29
  183.2 5.0 collective-permute-done.37.refs_5_
  191.1 6.1 collective-permute-done.38.refs_6_
  197.2 6.6 %collective-permute-done.39.refs_7_ = bf16[2,2,176,256]{3,2,1,0:T(8,128)(2,1)S(1)} collective-permute-done((bf16[2,2,176,256]{3,2,1,0:T(8,128)(2,1)}, bf16[2,2,176,256]{3,2,1,0:T(8,128)(2,1)S(1)}, u32[]{:S(2)}, u32[]{:S(2)}) %collective-permute-start.39) | collective-permute-done | bytes 360480 | tf_op jit(solution)/shard_map/ppermute | solution.py:29
  205.4 7.4 %all-to-all-start.1 = ((bf16[8,2,1,176,256]{4,3,2,1,0:T(8,128)(2,1)}), bf16[8,2,1,176,256]{4,3,2,1,0:T(8,128)(2,1)S(1)}, u32[]{:S(2)}, u32[]{:S(2)}) async-start(bf16[8,2,1,176,256]{4,3,2,1,0:T(8,128)(2,1)} %get-tuple-element.129), calls=%async_computation.1 | async-start | bytes 2883584 | tf_op jit(solution)/shard_map/all_to_all | solution.py:210
  215.3 50.3 %collective-permute-done.15.refs_4_ = bf16[2,3,176,256]{3,2,1,0:T(8,128)(2,1)} collective-permute-done((bf16[2,3,176,256]{3,2,1,0:T(8,128)(2,1)}, bf16[2,3,176,256]{3,2,1,0:T(8,128)(2,1)}, u32[]{:S(2)}, u32[]{:S(2)}) %collective-permute-start.15) | collective-permute-done | bytes 540704 | tf_op jit(solution)/shard_map/ppermute | solution.py:29
  266.3 10.9 %collective-permute-done.16.refs_5_ = bf16[2,3,176,256]{3,2,1,0:T(8,128)(2,1)} collective-permute-done((bf16[2,3,176,256]{3,2,1,0:T(8,128)(2,1)}, bf16[2,3,176,256]{3,2,1,0:T(8,128)(2,1)}, u32[]{:S(2)}, u32[]{:S(2)}) %collective-permute-start.16) | collective-permute-done | bytes 540704 | tf_op jit(solution)/shard_map/ppermute | solution.py:29
  277.9 12.2 %collective-permute-done.17.refs_6_ = bf16[2,3,176,256]{3,2,1,0:T(8,128)(2,1)} collective-permute-done((bf16[2,3,176,256]{3,2,1,0:T(8,128)(2,1)}, bf16[2,3,176,256]{3,2,1,0:T(8,128)(2,1)}, u32[]{:S(2)}, u32[]{:S(2)}) %collective-permute-start.17) | collective-permute-done | bytes 540704 | tf_op jit(solution)/shard_map/ppermute | solution.py:29
  290.1 67.6 %collective-permute-done.18.refs_7_ = bf16[2,3,176,256]{3,2,1,0:T(8,128)(2,1)S(1)} collective-permute-done((bf16[2,3,176,256]{3,2,1,0:T(8,128)(2,1)}, bf16[2,3,176,256]{3,2,1,0:T(8,128)(2,1)S(1)}, u32[]{:S(2)}, u32[]{:S(2)}) %collective-permute-start.18) | collective-permute-done | bytes 540704 | tf_op jit(solution)/shard_map/ppermute | solution.py:29
  360.1 4.2 collective-permute-start.20
  364.3 56.7 %collective-permute-done.30.refs_5_ = bf16[2,4,176,256]{3,2,1,0:T(8,128)(2,1)} collective-permute-done((bf16[2,4,176,256]{3,2,1,0:T(8,128)(2,1)}, bf16[2,4,176,256]{3,2,1,0:T(8,128)(2,1)}, u32[]{:S(2)}, u32[]{:S(2)}) %collective-permute-start.30) | collective-permute-done | bytes 720928 | tf_op jit(solution)/shard_map/ppermute | solution.py:29
  423.0 14.3 %collective-permute-done.31.refs_6_ = bf16[2,4,176,256]{3,2,1,0:T(8,128)(2,1)} collective-permute-done((bf16[2,4,176,256]{3,2,1,0:T(8,128)(2,1)}, bf16[2,4,176,256]{3,2,1,0:T(8,128)(2,1)}, u32[]{:S(2)}, u32[]{:S(2)}) %collective-permute-start.31) | collective-permute-done | bytes 720928 | tf_op jit(solution)/shard_map/ppermute | solution.py:29
  437.3 31.2 %collective-permute-done.32.refs_7_ = bf16[2,4,176,256]{3,2,1,0:T(8,128)(2,1)} collective-permute-done((bf16[2,4,176,256]{3,2,1,0:T(8,128)(2,1)}, bf16[2,4,176,256]{3,2,1,0:T(8,128)(2,1)}, u32[]{:S(2)}, u32[]{:S(2)}) %collective-permute-start.32) | collective-permute-done | bytes 720928 | tf_op jit(solution)/shard_map/ppermute | solution.py:29
  472.8 4.7 collective-permute-start.7
  477.5 51.7 %collective-permute-done.22.refs_4_ = bf16[2,4,176,256]{3,2,1,0:T(8,128)(2,1)} collective-permute-done((bf16[2,4,176,256]{3,2,1,0:T(8,128)(2,1)}, bf16[2,4,176,256]{3,2,1,0:T(8,128)(2,1)}, u32[]{:S(2)}, u32[]{:S(2)}) %collective-permute-start.22) | collective-permute-done | bytes 720928 | tf_op jit(solution)/shard_map/ppermute | solution.py:29
  532.5 15.9 %collective-permute-done.23.refs_5_ = bf16[2,4,176,256]{3,2,1,0:T(8,128)(2,1)} collective-permute-done((bf16[2,4,176,256]{3,2,1,0:T(8,128)(2,1)}, bf16[2,4,176,256]{3,2,1,0:T(8,128)(2,1)}, u32[]{:S(2)}, u32[]{:S(2)}) %collective-permute-start.23) | collective-permute-done | bytes 720928 | tf_op jit(solution)/shard_map/ppermute | solution.py:29
  551.5 24.8 %collective-permute-done.24.refs_6_ = bf16[2,4,176,256]{3,2,1,0:T(8,128)(2,1)} collective-permute-done((bf16[2,4,176,256]{3,2,1,0:T(8,128)(2,1)}, bf16[2,4,176,256]{3,2,1,0:T(8,128)(2,1)}, u32[]{:S(2)}, u32[]{:S(2)}) %collective-permute-start.24) | collective-permute-done | bytes 720928 | tf_op jit(solution)/shard_map/ppermute | solution.py:29
  578.0 14.1 %collective-permute-done.25.refs_7_ = bf16[2,4,176,256]{3,2,1,0:T(8,128)(2,1)} collective-permute-done((bf16[2,4,176,256]{3,2,1,0:T(8,128)(2,1)}, bf16[2,4,176,256]{3,2,1,0:T(8,128)(2,1)}, u32[]{:S(2)}, u32[]{:S(2)}) %collective-permute-start.25) | collective-permute-done | bytes 720928 | tf_op jit(solution)/shard_map/ppermute | solution.py:29
  604.0 10.6 %all_gather.3.x = bf16[64,2048]{1,0:T(8,128)(2,1)} all-gather(bf16[16,2048]{1,0:T(8,128)(2,1)} %join.1), channel_id=1, replica_groups=mesh['ep'=4,'fsdp'=8] {'ep'}, dimensions={0}, use_global_device_ids=true | all-gather | bytes 327680 | tf_op jit(solution)/shard_map/all_gather | solution.py:242
  619.4 5.8 place.10
  625.3 5.8 place.11
  631.1 5.3 place.12
  (191 shorter events, 109.4 us)
Async XLA Ops:
  73.9 57.2 %collective-permute-start.45 = (bf16[2,1,176,256]{3,2,1,0:T(8,128)(2,1)}, bf16[2,1,176,256]{3,2,1,0:T(8,128)(2,1)S(1)}, u32[]{:S(2)}, u32[]{:S(2)}) collective-permute-start(bf16[2,1,176,256]{3,2,1,0:T(8,128)(2,1)} %get-tuple-element.127), channel_id=1, source_target_pairs={{0,6},{1,7},{2,4},{3,5},{4,2},{5,3},{6,0},{7,1},{8,14},{9,15},{10,... | collective-permute-start | bytes 540680 | tf_op jit(solution)/shard_map/ppermute | solution.py:29
  79.2 53.0 %collective-permute-start.46 = (bf16[2,1,176,256]{3,2,1,0:T(8,128)(2,1)}, bf16[2,1,176,256]{3,2,1,0:T(8,128)(2,1)S(1)}, u32[]{:S(2)}, u32[]{:S(2)}) collective-permute-start(bf16[2,1,176,256]{3,2,1,0:T(8,128)(2,1)} %get-tuple-element.128), channel_id=1, source_target_pairs={{0,7},{1,6},{2,5},{3,4},{4,3},{5,2},{6,1},{7,0},{8,15},{9,14},{10,... | collective-permute-start | bytes 540680 | tf_op jit(solution)/shard_map/ppermute | solution.py:29
  85.2 55.6 %collective-permute-start.33 = (bf16[2,2,176,256]{3,2,1,0:T(8,128)(2,1)}, bf16[2,2,176,256]{3,2,1,0:T(8,128)(2,1)S(1)}, u32[]{:S(2)}, u32[]{:S(2)}) collective-permute-start(bf16[2,2,176,256]{3,2,1,0:T(8,128)(2,1)} %get-tuple-element.114), channel_id=1, source_target_pairs={{0,1},{1,0},{2,3},{3,2},{4,5},{5,4},{6,7},{7,6},{8,9},{9,8},{10,11... | collective-permute-start | bytes 1081352 | tf_op jit(solution)/shard_map/ppermute | solution.py:29
  86.1 55.7 %collective-permute-start.34 = (bf16[2,2,176,256]{3,2,1,0:T(8,128)(2,1)}, bf16[2,2,176,256]{3,2,1,0:T(8,128)(2,1)S(1)}, u32[]{:S(2)}, u32[]{:S(2)}) collective-permute-start(bf16[2,2,176,256]{3,2,1,0:T(8,128)(2,1)} %get-tuple-element.115), channel_id=1, source_target_pairs={{0,2},{1,3},{2,0},{3,1},{4,6},{5,7},{6,4},{7,5},{8,10},{9,11},{10,... | collective-permute-start | bytes 1081352 | tf_op jit(solution)/shard_map/ppermute | solution.py:29
  98.1 45.0 %collective-permute-start.35 = (bf16[2,2,176,256]{3,2,1,0:T(8,128)(2,1)}, bf16[2,2,176,256]{3,2,1,0:T(8,128)(2,1)S(1)}, u32[]{:S(2)}, u32[]{:S(2)}) collective-permute-start(bf16[2,2,176,256]{3,2,1,0:T(8,128)(2,1)} %get-tuple-element.116), channel_id=1, source_target_pairs={{0,3},{1,2},{2,1},{3,0},{4,7},{5,6},{6,5},{7,4},{8,11},{9,10},{10,... | collective-permute-start | bytes 1081352 | tf_op jit(solution)/shard_map/ppermute | solution.py:29
  133.5 70.4 %collective-permute-start.12 = (bf16[2,3,176,256]{3,2,1,0:T(8,128)(2,1)}, bf16[2,3,176,256]{3,2,1,0:T(8,128)(2,1)S(1)}, u32[]{:S(2)}, u32[]{:S(2)}) collective-permute-start(bf16[2,3,176,256]{3,2,1,0:T(8,128)(2,1)} %get-tuple-element.90), channel_id=1, source_target_pairs={{0,1},{1,0},{2,3},{3,2},{4,5},{5,4},{6,7},{7,6},{8,9},{9,8},{10,11... | collective-permute-start | bytes 1622024 | tf_op jit(solution)/shard_map/ppermute | solution.py:29
  140.8 47.4 %collective-permute-start.37 = (bf16[2,2,176,256]{3,2,1,0:T(8,128)(2,1)S(1)}, bf16[2,2,176,256]{3,2,1,0:T(8,128)(2,1)S(1)}, u32[]{:S(2)}, u32[]{:S(2)}) collective-permute-start(bf16[2,2,176,256]{3,2,1,0:T(8,128)(2,1)S(1)} %copy-done.41), channel_id=1, source_target_pairs={{0,5},{1,4},{2,7},{3,6},{4,1},{5,0},{6,3},{7,2},{8,13},{9,12},{10,... | collective-permute-start | bytes 1081352 | tf_op jit(solution)/shard_map/ppermute | solution.py:29
  141.9 55.4 %collective-permute-start.38 = (bf16[2,2,176,256]{3,2,1,0:T(8,128)(2,1)}, bf16[2,2,176,256]{3,2,1,0:T(8,128)(2,1)S(1)}, u32[]{:S(2)}, u32[]{:S(2)}) collective-permute-start(bf16[2,2,176,256]{3,2,1,0:T(8,128)(2,1)} %get-tuple-element.119), channel_id=1, source_target_pairs={{0,6},{1,7},{2,4},{3,5},{4,2},{5,3},{6,0},{7,1},{8,14},{9,15},{10,... | collective-permute-start | bytes 1081352 | tf_op jit(solution)/shard_map/ppermute | solution.py:29
  143.1 60.8 %collective-permute-start.39 = (bf16[2,2,176,256]{3,2,1,0:T(8,128)(2,1)}, bf16[2,2,176,256]{3,2,1,0:T(8,128)(2,1)S(1)}, u32[]{:S(2)}, u32[]{:S(2)}) collective-permute-start(bf16[2,2,176,256]{3,2,1,0:T(8,128)(2,1)} %get-tuple-element.120), channel_id=1, source_target_pairs={{0,7},{1,6},{2,5},{3,4},{4,3},{5,2},{6,1},{7,0},{8,15},{9,14},{10,... | collective-permute-start | bytes 1081352 | tf_op jit(solution)/shard_map/ppermute | solution.py:29
  197.2 68.4 %collective-permute-start.15 = (bf16[2,3,176,256]{3,2,1,0:T(8,128)(2,1)}, bf16[2,3,176,256]{3,2,1,0:T(8,128)(2,1)}, u32[]{:S(2)}, u32[]{:S(2)}) collective-permute-start(bf16[2,3,176,256]{3,2,1,0:T(8,128)(2,1)} %get-tuple-element.93), channel_id=1, source_target_pairs={{0,4},{1,5},{2,6},{3,7},{4,0},{5,1},{6,2},{7,3},{8,12},{9,13},{10,... | collective-permute-start | bytes 1622024 | tf_op jit(solution)/shard_map/ppermute | solution.py:29
  203.8 73.4 %collective-permute-start.16 = (bf16[2,3,176,256]{3,2,1,0:T(8,128)(2,1)}, bf16[2,3,176,256]{3,2,1,0:T(8,128)(2,1)}, u32[]{:S(2)}, u32[]{:S(2)}) collective-permute-start(bf16[2,3,176,256]{3,2,1,0:T(8,128)(2,1)} %get-tuple-element.94), channel_id=1, source_target_pairs={{0,5},{1,4},{2,7},{3,6},{4,1},{5,0},{6,3},{7,2},{8,13},{9,12},{10,... | collective-permute-start | bytes 1622024 | tf_op jit(solution)/shard_map/ppermute | solution.py:29
  204.6 85.5 %collective-permute-start.17 = (bf16[2,3,176,256]{3,2,1,0:T(8,128)(2,1)}, bf16[2,3,176,256]{3,2,1,0:T(8,128)(2,1)}, u32[]{:S(2)}, u32[]{:S(2)}) collective-permute-start(bf16[2,3,176,256]{3,2,1,0:T(8,128)(2,1)} %get-tuple-element.95), channel_id=1, source_target_pairs={{0,6},{1,7},{2,4},{3,5},{4,2},{5,3},{6,0},{7,1},{8,14},{9,15},{10,... | collective-permute-start | bytes 1622024 | tf_op jit(solution)/shard_map/ppermute | solution.py:29
  205.4 390.6 %all-to-all-start.1 = ((bf16[8,2,1,176,256]{4,3,2,1,0:T(8,128)(2,1)}), bf16[8,2,1,176,256]{4,3,2,1,0:T(8,128)(2,1)S(1)}, u32[]{:S(2)}, u32[]{:S(2)}) async-start(bf16[8,2,1,176,256]{4,3,2,1,0:T(8,128)(2,1)} %get-tuple-element.129), calls=%async_computation.1 | async-start | bytes 2883584 | tf_op jit(solution)/shard_map/all_to_all | solution.py:210
  213.6 144.2 %collective-permute-start.26 = (bf16[2,4,176,256]{3,2,1,0:T(8,128)(2,1)}, bf16[2,4,176,256]{3,2,1,0:T(8,128)(2,1)S(1)}, u32[]{:S(2)}, u32[]{:S(2)}) collective-permute-start(bf16[2,4,176,256]{3,2,1,0:T(8,128)(2,1)} %get-tuple-element.106), channel_id=1, source_target_pairs={{0,1},{1,0},{2,3},{3,2},{4,5},{5,4},{6,7},{7,6},{8,9},{9,8},{10,11... | collective-permute-start | bytes 2162696 | tf_op jit(solution)/shard_map/ppermute | solution.py:29
  214.5 143.9 %collective-permute-start.27 = (bf16[2,4,176,256]{3,2,1,0:T(8,128)(2,1)}, bf16[2,4,176,256]{3,2,1,0:T(8,128)(2,1)S(1)}, u32[]{:S(2)}, u32[]{:S(2)}) collective-permute-start(bf16[2,4,176,256]{3,2,1,0:T(8,128)(2,1)} %get-tuple-element.107), channel_id=1, source_target_pairs={{0,2},{1,3},{2,0},{3,1},{4,6},{5,7},{6,4},{7,5},{8,10},{9,11},{10,... | collective-permute-start | bytes 2162696 | tf_op jit(solution)/shard_map/ppermute | solution.py:29
  265.7 94.3 %collective-permute-start.28 = (bf16[2,4,176,256]{3,2,1,0:T(8,128)(2,1)}, bf16[2,4,176,256]{3,2,1,0:T(8,128)(2,1)}, u32[]{:S(2)}, u32[]{:S(2)}) collective-permute-start(bf16[2,4,176,256]{3,2,1,0:T(8,128)(2,1)} %get-tuple-element.108), channel_id=1, source_target_pairs={{0,3},{1,2},{2,1},{3,0},{4,7},{5,6},{6,5},{7,4},{8,11},{9,10},{10,... | collective-permute-start | bytes 2162696 | tf_op jit(solution)/shard_map/ppermute | solution.py:29
  277.3 82.8 %collective-permute-start.29 = (bf16[2,4,176,256]{3,2,1,0:T(8,128)(2,1)}, bf16[2,4,176,256]{3,2,1,0:T(8,128)(2,1)}, u32[]{:S(2)}, u32[]{:S(2)}) collective-permute-start(bf16[2,4,176,256]{3,2,1,0:T(8,128)(2,1)} %get-tuple-element.109), channel_id=1, source_target_pairs={{0,4},{1,5},{2,6},{3,7},{4,0},{5,1},{6,2},{7,3},{8,12},{9,13},{10,... | collective-permute-start | bytes 2162696 | tf_op jit(solution)/shard_map/ppermute | solution.py:29
  290.1 67.7 %collective-permute-start.18 = (bf16[2,3,176,256]{3,2,1,0:T(8,128)(2,1)}, bf16[2,3,176,256]{3,2,1,0:T(8,128)(2,1)S(1)}, u32[]{:S(2)}, u32[]{:S(2)}) collective-permute-start(bf16[2,3,176,256]{3,2,1,0:T(8,128)(2,1)} %get-tuple-element.96), channel_id=1, source_target_pairs={{0,7},{1,6},{2,5},{3,4},{4,3},{5,2},{6,1},{7,0},{8,15},{9,14},{10,... | collective-permute-start | bytes 1622024 | tf_op jit(solution)/shard_map/ppermute | solution.py:29
  357.8 63.2 %collective-permute-start.30 = (bf16[2,4,176,256]{3,2,1,0:T(8,128)(2,1)}, bf16[2,4,176,256]{3,2,1,0:T(8,128)(2,1)}, u32[]{:S(2)}, u32[]{:S(2)}) collective-permute-start(bf16[2,4,176,256]{3,2,1,0:T(8,128)(2,1)} %get-tuple-element.110), channel_id=1, source_target_pairs={{0,5},{1,4},{2,7},{3,6},{4,1},{5,0},{6,3},{7,2},{8,13},{9,12},{10,... | collective-permute-start | bytes 2162696 | tf_op jit(solution)/shard_map/ppermute | solution.py:29
  357.8 79.5 %collective-permute-start.31 = (bf16[2,4,176,256]{3,2,1,0:T(8,128)(2,1)}, bf16[2,4,176,256]{3,2,1,0:T(8,128)(2,1)}, u32[]{:S(2)}, u32[]{:S(2)}) collective-permute-start(bf16[2,4,176,256]{3,2,1,0:T(8,128)(2,1)} %get-tuple-element.111), channel_id=1, source_target_pairs={{0,6},{1,7},{2,4},{3,5},{4,2},{5,3},{6,0},{7,1},{8,14},{9,15},{10,... | collective-permute-start | bytes 2162696 | tf_op jit(solution)/shard_map/ppermute | solution.py:29
  358.6 110.0 %collective-permute-start.32 = (bf16[2,4,176,256]{3,2,1,0:T(8,128)(2,1)}, bf16[2,4,176,256]{3,2,1,0:T(8,128)(2,1)}, u32[]{:S(2)}, u32[]{:S(2)}) collective-permute-start(bf16[2,4,176,256]{3,2,1,0:T(8,128)(2,1)} %get-tuple-element.112), channel_id=1, source_target_pairs={{0,7},{1,6},{2,5},{3,4},{4,3},{5,2},{6,1},{7,0},{8,15},{9,14},{10,... | collective-permute-start | bytes 2162696 | tf_op jit(solution)/shard_map/ppermute | solution.py:29
  360.0 108.5 %collective-permute-start.19 = (bf16[2,4,176,256]{3,2,1,0:T(8,128)(2,1)}, bf16[2,4,176,256]{3,2,1,0:T(8,128)(2,1)}, u32[]{:S(2)}, u32[]{:S(2)}) collective-permute-start(bf16[2,4,176,256]{3,2,1,0:T(8,128)(2,1)} %get-tuple-element.98), channel_id=1, source_target_pairs={{0,1},{1,0},{2,3},{3,2},{4,5},{5,4},{6,7},{7,6},{8,9},{9,8},{10,11... | collective-permute-start | bytes 2162696 | tf_op jit(solution)/shard_map/ppermute | solution.py:29
  360.1 109.8 %collective-permute-start.20 = (bf16[2,4,176,256]{3,2,1,0:T(8,128)(2,1)}, bf16[2,4,176,256]{3,2,1,0:T(8,128)(2,1)}, u32[]{:S(2)}, u32[]{:S(2)}) collective-permute-start(bf16[2,4,176,256]{3,2,1,0:T(8,128)(2,1)} %get-tuple-element.99), channel_id=1, source_target_pairs={{0,2},{1,3},{2,0},{3,1},{4,6},{5,7},{6,4},{7,5},{8,10},{9,11},{10,... | collective-permute-start | bytes 2162696 | tf_op jit(solution)/shard_map/ppermute | solution.py:29
  421.0 51.8 %collective-permute-start.21 = (bf16[2,4,176,256]{3,2,1,0:T(8,128)(2,1)}, bf16[2,4,176,256]{3,2,1,0:T(8,128)(2,1)}, u32[]{:S(2)}, u32[]{:S(2)}) collective-permute-start(bf16[2,4,176,256]{3,2,1,0:T(8,128)(2,1)} %get-tuple-element.100), channel_id=1, source_target_pairs={{0,3},{1,2},{2,1},{3,0},{4,7},{5,6},{6,5},{7,4},{8,11},{9,10},{10,... | collective-permute-start | bytes 2162696 | tf_op jit(solution)/shard_map/ppermute | solution.py:29
  437.3 91.9 %collective-permute-start.22 = (bf16[2,4,176,256]{3,2,1,0:T(8,128)(2,1)}, bf16[2,4,176,256]{3,2,1,0:T(8,128)(2,1)}, u32[]{:S(2)}, u32[]{:S(2)}) collective-permute-start(bf16[2,4,176,256]{3,2,1,0:T(8,128)(2,1)} %get-tuple-element.101), channel_id=1, source_target_pairs={{0,4},{1,5},{2,6},{3,7},{4,0},{5,1},{6,2},{7,3},{8,12},{9,13},{10,... | collective-permute-start | bytes 2162696 | tf_op jit(solution)/shard_map/ppermute | solution.py:29
  468.5 79.9 %collective-permute-start.23 = (bf16[2,4,176,256]{3,2,1,0:T(8,128)(2,1)}, bf16[2,4,176,256]{3,2,1,0:T(8,128)(2,1)}, u32[]{:S(2)}, u32[]{:S(2)}) collective-permute-start(bf16[2,4,176,256]{3,2,1,0:T(8,128)(2,1)} %get-tuple-element.102), channel_id=1, source_target_pairs={{0,5},{1,4},{2,7},{3,6},{4,1},{5,0},{6,3},{7,2},{8,13},{9,12},{10,... | collective-permute-start | bytes 2162696 | tf_op jit(solution)/shard_map/ppermute | solution.py:29
  468.5 107.8 %collective-permute-start.24 = (bf16[2,4,176,256]{3,2,1,0:T(8,128)(2,1)}, bf16[2,4,176,256]{3,2,1,0:T(8,128)(2,1)}, u32[]{:S(2)}, u32[]{:S(2)}) collective-permute-start(bf16[2,4,176,256]{3,2,1,0:T(8,128)(2,1)} %get-tuple-element.103), channel_id=1, source_target_pairs={{0,6},{1,7},{2,4},{3,5},{4,2},{5,3},{6,0},{7,1},{8,14},{9,15},{10,... | collective-permute-start | bytes 2162696 | tf_op jit(solution)/shard_map/ppermute | solution.py:29
  469.9 122.2 %collective-permute-start.25 = (bf16[2,4,176,256]{3,2,1,0:T(8,128)(2,1)}, bf16[2,4,176,256]{3,2,1,0:T(8,128)(2,1)}, u32[]{:S(2)}, u32[]{:S(2)}) collective-permute-start(bf16[2,4,176,256]{3,2,1,0:T(8,128)(2,1)} %get-tuple-element.104), channel_id=1, source_target_pairs={{0,7},{1,6},{2,5},{3,4},{4,3},{5,2},{6,1},{7,0},{8,15},{9,14},{10,... | collective-permute-start | bytes 2162696 | tf_op jit(solution)/shard_map/ppermute | solution.py:29
  472.8 163.6 %collective-permute-start.7 = (bf16[2,1,176,256]{3,2,1,0:T(8,128)(2,1)}, bf16[2,1,176,256]{3,2,1,0:T(8,128)(2,1)}, u32[]{:S(2)}, u32[]{:S(2)}) collective-permute-start(bf16[2,1,176,256]{3,2,1,0:T(8,128)(2,1)} %get-tuple-element.84), channel_id=1, source_target_pairs={{0,3},{1,2},{2,1},{3,0},{4,7},{5,6},{6,5},{7,4},{8,11},{9,10},{10,... | collective-permute-start | bytes 540680 | tf_op jit(solution)/shard_map/ppermute | solution.py:29
  529.1 107.3 %collective-permute-start.8 = (bf16[2,1,176,256]{3,2,1,0:T(8,128)(2,1)}, bf16[2,1,176,256]{3,2,1,0:T(8,128)(2,1)}, u32[]{:S(2)}, u32[]{:S(2)}) collective-permute-start(bf16[2,1,176,256]{3,2,1,0:T(8,128)(2,1)} %get-tuple-element.85), channel_id=1, source_target_pairs={{0,4},{1,5},{2,6},{3,7},{4,0},{5,1},{6,2},{7,3},{8,12},{9,13},{10,... | collective-permute-start | bytes 540680 | tf_op jit(solution)/shard_map/ppermute | solution.py:29
  548.4 88.0 %collective-permute-start.9 = (bf16[2,1,176,256]{3,2,1,0:T(8,128)(2,1)}, bf16[2,1,176,256]{3,2,1,0:T(8,128)(2,1)}, u32[]{:S(2)}, u32[]{:S(2)}) collective-permute-start(bf16[2,1,176,256]{3,2,1,0:T(8,128)(2,1)} %get-tuple-element.86), channel_id=1, source_target_pairs={{0,5},{1,4},{2,7},{3,6},{4,1},{5,0},{6,3},{7,2},{8,13},{9,12},{10,... | collective-permute-start | bytes 540680 | tf_op jit(solution)/shard_map/ppermute | solution.py:29
  576.3 60.1 %collective-permute-start.10 = (bf16[2,1,176,256]{3,2,1,0:T(8,128)(2,1)}, bf16[2,1,176,256]{3,2,1,0:T(8,128)(2,1)}, u32[]{:S(2)}, u32[]{:S(2)}) collective-permute-start(bf16[2,1,176,256]{3,2,1,0:T(8,128)(2,1)} %get-tuple-element.87), channel_id=1, source_target_pairs={{0,6},{1,7},{2,4},{3,5},{4,2},{5,3},{6,0},{7,1},{8,14},{9,15},{10,... | collective-permute-start | bytes 540680 | tf_op jit(solution)/shard_map/ppermute | solution.py:29
  (67 other events, 2973.1 us)
